TPU v7x, 32 devices: a whole 2x2x4 slice. The times are simulated.
32 devices in a mesh: dp: 4 (over x, y), tp: 8 (over z, core).
Axes of the slice: x: 2, y: 2, z: 4, core: 2. Of those that a mesh axis runs over, the one named last changes fastest.
Arguments:
- x: bfloat16 [8192, 4096], P('dp'), parts along dimension 0
- dy: bfloat16 [8192, 4096], P('dp'), parts along dimension 0
- gate: bfloat16 [8192, 16384], P('dp', 'tp'), parts along dimension 0
- up: bfloat16 [8192, 16384], P('dp', 'tp'), parts along dimension 0
- w_gate: bfloat16 [4096, 16384], P(None, 'tp')
- w_up: bfloat16 [4096, 16384], P(None, 'tp')
- w_down: bfloat16 [16384, 4096], P('tp')
Outputs:
- output 1: bfloat16 [8192, 4096], P('dp'), parts along dimension 0
- output 2: bfloat16 [16384, 16384], P('dp', 'tp'), parts along dimension 0
- output 3: bfloat16 [16384, 16384], P('dp', 'tp'), parts along dimension 0
- output 4: bfloat16 [65536, 4096], P(('dp', 'tp')), parts along dimension 0
There are 4 independent parts. A program takes and returns all parts, laid end to end along the dimension named above; an argument that names none is the same for every part.
All inputs are finite; a program needn't handle non-finite values.
Results may differ from a plain program's by a relative error of at most 0.012.
Values are sent between devices in bfloat16 or wider.
A program may use at most 2 GiB of HBM per device.

v0:
```python
import jax
import jax.numpy as jnp
from jax import lax
from jax.sharding import PartitionSpec as P


def act(gate, up):
    return jax.nn.silu(gate) * up


def solution(mesh):
    def step(x, dy, gate, up, w_gate, w_up, w_down):
        hidden, back = jax.vjp(act, gate.astype(jnp.float32), up.astype(jnp.float32))
        d_hidden = jnp.dot(dy, w_down.T, preferred_element_type=jnp.float32)
        d_gate, d_up = (g.astype(jnp.bfloat16) for g in back(d_hidden))
        term = jnp.dot(d_gate, w_gate.T, preferred_element_type=jnp.float32) + jnp.dot(d_up, w_up.T, preferred_element_type=jnp.float32)
        dx = lax.psum(term.astype(jnp.bfloat16), "tp")
        dw_gate = jnp.dot(x.T, d_gate, preferred_element_type=jnp.float32)
        dw_up = jnp.dot(x.T, d_up, preferred_element_type=jnp.float32)
        dw_down = jnp.dot(hidden.astype(jnp.bfloat16).T, dy, preferred_element_type=jnp.float32)
        return dx, *(g.astype(jnp.bfloat16) for g in (dw_gate, dw_up, dw_down))

    tokens, columns, rows = P("dp", None), P(None, "tp"), P("tp", None)
    return jax.shard_map(
        step,
        mesh=mesh,
        in_specs=(tokens, tokens, P("dp", "tp"), P("dp", "tp"), columns, columns, rows),
        out_specs=(tokens, P("dp", "tp"), P("dp", "tp"), P(("dp", "tp"), None)),
        check_vma=False,
    )
```

profile of v0, /device:TPU:0, one launch (start us, length us, event | category | flops | bytes accessed | tf_op | source)
XLA Modules:
  0.0 519.5 jit_solution(11452642854368146354)
XLA Ops:
  7.2 0.0 all-reduce.2.cloned.1.call-start
  7.2 53.5 %fusion.6 = (bf16[2048,2048]{1,0:T(8,128)(2,1)}, f32[2048,2048]{1,0:T(8,128)}) fusion(bf16[2048,2048]{1,0:T(8,128)(2,1)} %param.9, bf16[2048,2048]{1,0:T(8,128)(2,1)} %param.10, bf16[2048,4096]{1,0:T(8,128)(2,1)} %param.8, bf16[2048,4096]{1,0:T(8,128)(2,1)} %param.13), kind=kOutput, calls=%fused_computation.13 | convolution fusion | flops 34414264320 | bytes 75497472 | tf_op jit(solution)/shard_map/dot_general | solution.py:14
  60.7 43.7 %fusion.9 = f32[2048,4096]{1,0:T(8,128)} fusion(bf16[2048,2048]{1,0:T(8,128)(2,1)} %get-tuple-element.8, bf16[4096,2048]{1,0:T(8,128)(2,1)} %param.11), kind=kOutput, calls=%fused_computation.19 | convolution fusion | flops 34359738368 | bytes 58720256 | tf_op jit(solution)/shard_map/dot_general | solution.py:16
  104.4 58.1 %add_convert_fusion = bf16[2048,4096]{1,0:T(8,128)(2,1)} fusion(f32[2048,4096]{1,0:T(8,128)} %fusion.9, bf16[4096,2048]{1,0:T(8,128)(2,1)} %param.12, f32[2048,2048]{1,0:T(8,128)} %get-tuple-element.9, bf16[2048,2048]{1,0:T(8,128)(2,1)} %param.9), kind=kOutput, calls=%fused_computation | convolution fusion | flops 34405875712 | bytes 92274688 | tf_op jit(solution)/shard_map/dot_general | solution.py:16
  162.5 0.0 all-reduce.2.cloned.1.call-update
  162.6 42.0 %convert_bitcast_fusion.1 = bf16[4096,2048]{0,1:T(8,128)(2,1)} fusion(bf16[2048,2048]{1,0:T(8,128)(2,1)} %get-tuple-element.8, bf16[2048,4096]{1,0:T(8,128)(2,1)} %param.7), kind=kOutput, calls=%fused_computation.15 | convolution fusion | flops 34368126976 | bytes 41943040 | tf_op jit(solution)/shard_map/dot_general | solution.py:18
  204.6 47.5 %convert_bitcast_fusion = bf16[4096,2048]{0,1:T(8,128)(2,1)} fusion(bf16[2048,4096]{1,0:T(8,128)(2,1)} %param.7, f32[2048,2048]{1,0:T(8,128)} %get-tuple-element.9, bf16[2048,2048]{1,0:T(8,128)(2,1)} %param.9), kind=kOutput, calls=%fused_computation.14 | convolution fusion | flops 34397487104 | bytes 58720256 | tf_op jit(solution)/shard_map/dot_general | solution.py:19
  252.1 22.4 %copy.11 = bf16[4096,2048]{1,0:T(8,128)(2,1)} copy(bf16[4096,2048]{0,1:T(8,128)(2,1)} %convert_bitcast_fusion.1) | data formatting | bytes 33554432
  274.5 22.4 %copy.12 = bf16[4096,2048]{1,0:T(8,128)(2,1)} copy(bf16[4096,2048]{0,1:T(8,128)(2,1)} %convert_bitcast_fusion) | data formatting | bytes 33554432
  296.9 47.5 %convolution_convert_fusion = bf16[2048,4096]{1,0:T(8,128)(2,1)} fusion(bf16[2048,4096]{1,0:T(8,128)(2,1)} %param.8, bf16[2048,2048]{1,0:T(8,128)(2,1)} %param.10, bf16[2048,2048]{1,0:T(8,128)(2,1)} %param.9), kind=kOutput, calls=%fused_computation.17 | convolution fusion | flops 34401681408 | bytes 50331648 | tf_op jit(solution)/shard_map/dot_general | solution.py:20
  344.4 153.7 %all-reduce.2.cloned.1.call-done = bf16[2048,4096]{1,0:T(8,128)(2,1)} async-done(((bf16[2048,4096]{1,0:T(8,128)(2,1)}), bf16[2048,4096]{1,0:T(8,128)(2,1)}) %all-reduce.2.cloned.1.call-update) | async-done | bytes 16777232 | tf_op jit(solution)/shard_map/psum | solution.py:17
  498.1 14.1 %copy.14 = bf16[2048,4096]{1,0:T(8,128)(2,1)} copy(bf16[2048,4096]{1,0:T(8,128)(2,1)} %all-reduce.2.cloned.1.call-done) | data formatting | bytes 33554432
Async XLA Ops:
  7.2 490.9 %all-reduce.2.cloned.1.call-start = ((), (), s32[]{:S(2)}) async-start(), calls=%async_computation | async-start | bytes 33554432 | tf_op jit(solution)/shard_map/psum | solution.py:17
Sparse Core Ops, SparseCore 0:
  162.7 335.3 all-reduce.1
where the time goes:
time: 528 us; the launch traced here: 519 us
  matrix products  292 us (55%)
  waiting for transfers between devices  154 us (29%)
  local copies, waits for them, and re-layouts  58.9 us (11%)
  between operations  14.5 us (3%)
    psum x1, waiting for transfers between devices, step(): dx = lax.psum(term.astype(jnp.bfloat16), 'tp')  154 us
    unnamed x3, local copies, waits for them, and re-layouts  58.9 us
    dot_general x1, matrix products, step(): jnp.dot(d_up, w_up.T, preferred_element_type=jnp.float32)  58.1 us
    dot_general x1, matrix products, step(): d_hidden = jnp.dot(dy, w_down.T, preferred_element_type=jnp.float32)  53.5 us
    dot_general x1, matrix products, step(): dw_up = jnp.dot(x.T, d_up, preferred_element_type=jnp.float32)  47.5 us
    dot_general x1, matrix products, step(): jnp.dot(hidden.astype(jnp.bfloat16).T, dy, preferred_element_type=jnp.flo...  47.5 us
    dot_general x1, matrix products, step(): jnp.dot(d_gate, w_gate.T, preferred_element_type=jnp.float32)  43.7 us
    dot_general x1, matrix products, step(): dw_gate = jnp.dot(x.T, d_gate, preferred_element_type=jnp.float32)  42 us
  transfers between devices with their start and end apart: 1, of which 1 were waited for; matrix products, arithmetic and copies ran while one was open for 35% of the time, Pallas kernels for 0%

commit v1 on v0

v1 whole, which is shorter than its diff:
```python
import jax
import jax.numpy as jnp
from jax import lax
from jax.experimental import pallas as pl
from jax.experimental.pallas import tpu as pltpu
from jax.sharding import PartitionSpec as P

f32, bf = jnp.float32, jnp.bfloat16
NT = (((1,), (1,)), ((), ()))
TN = (((0,), (0,)), ((), ()))
MESH = pl.DeviceIdType.MESH
ANY = pl.BlockSpec(memory_space=pl.ANY)

T, D, F = 2048, 4096, 2048
R = 512
N = 1024
H = R // 2
NP1 = 24
NW = 16
NB = 16
K0 = 5
LAST = NP1 + NW
END = LAST + 3


def ds(start, size):
    return pl.ds(start if isinstance(start, int) else pl.multiple_of(start, size), size)


def copy(a, b, s):
    return pltpu.make_async_copy(a, b, s)


def start(copies):
    for c in copies:
        c.start()


def wait(copies):
    for c in copies:
        c.wait()


def kernel_a(x, dy, gate, up, wg, wu, wd, dgu, hid, dwg, dwu, dx,
             W, dyb, gub, dgb, Pb, Qb, Yb, Ib, Sb,
             semw, semi, semo, semd, r_i, s_i, r_x, s_x, r_y, s_y, r_f, s_fe, s_fm, r_p, s_p, s_l):
    t = lax.axis_index("tp")
    z, core = t // 2, t % 2
    peer = z * 2 + 1 - core
    edge = (z == 0) | (z == 3)
    outer = jnp.where(z < 2, core, 6 + core)
    inner = jnp.where(z < 2, 4 + core, 2 + core)
    mine = jnp.where(z < 2, 0, 1)
    theirs = 1 - mine
    middle = jnp.where(z < 2, 2 + core, 4 + core)

    def remote(a, b, s, r, to):
        return pltpu.make_async_remote_copy(a, b, s, r, device_id={"tp": to}, device_id_type=MESH)

    def loads_a(k, slot):
        i = k % 6
        return [copy(wd.at[ds(i * N, N), :], W.at[slot], semw.at[slot, 0])]

    def loads_b(k, slot):
        j = k % 6 - 2
        return [copy(wg.at[ds(j * N, N), :], W.at[slot, :, pl.ds(0, F)], semw.at[slot, 0]),
                copy(wu.at[ds(j * N, N), :], W.at[slot, :, pl.ds(F, F)], semw.at[slot, 1])]

    def loads_w(k, slot):
        i, j = (k - NP1) // 4, (k - NP1) % 4
        return [copy(x.at[pl.ds(0, N), ds(i * N, N)], W.at[slot, :, pl.ds(0, N)], semw.at[slot, 0]),
                copy(x.at[pl.ds(N, N), ds(i * N, N)], W.at[slot, :, pl.ds(N, N)], semw.at[slot, 1]),
                copy(dgu.at[pl.ds(0, N), ds(j * N, N)], W.at[slot, :, pl.ds(2 * N, N)], semw.at[slot, 2]),
                copy(dgu.at[pl.ds(N, N), ds(j * N, N)], W.at[slot, :, pl.ds(3 * N, N)], semw.at[slot, 3])]

    def in_loads(r):
        return [copy(dy.at[ds(r * R, R), :], dyb, semi.at[0]),
                copy(gate.at[ds(r * R, R), :], gub.at[0], semi.at[1]),
                copy(up.at[ds(r * R, R), :], gub.at[1], semi.at[2])]

    def outs_g(r):
        return [copy(dgb, dgu.at[ds(r * R, R), :], semo.at[0]),
                copy(gub.at[0], hid.at[ds(r * R, R), :], semo.at[1])]

    def outs_w(k, dst):
        slot, i, j = k % 2, (k - NP1) // 4, (k - NP1) % 2
        return [copy(dyb.at[:, ds(slot * 2 * N + h * N, N)],
                     dst.at[ds(i * N + h * R, R), ds(j * N, N)], semd.at[slot, h]) for h in range(2)]

    def kind(k):
        first = k < NP1
        return first & (k % 6 < 2), first & (k % 6 >= 2), jnp.logical_not(first) & (k < LAST)

    start(in_loads(0))
    start(loads_a(0, 0))
    barrier = pltpu.get_barrier_semaphore()
    pl.semaphore_signal(barrier, inc=1, device_id={"tp": peer}, device_id_type=MESH)

    @pl.when(edge)
    def _():
        pl.semaphore_signal(barrier, inc=1, device_id={"tp": middle}, device_id_type=MESH)

    @pl.when(jnp.logical_not(edge))
    def _():
        pl.semaphore_signal(barrier, inc=1, device_id={"tp": outer}, device_id_type=MESH)
        pl.semaphore_signal(barrier, inc=1, device_id={"tp": inner}, device_id_type=MESH)
    pl.semaphore_wait(barrier, jnp.where(edge, 2, 3))

    def region(b, c, h):
        return dx.at[ds((b // 4) * R + c * H, H), ds((b % 4) * N + h * R, R)]

    def pair_send(b):
        s = b % 2
        return remote(Sb.at[s], Ib.at[s], s_i.at[s], r_i.at[s], peer)

    def x_send(b, h):
        return remote(Qb.at[b, h], Qb.at[b, h], s_x.at[h, b], r_x.at[h, b], middle)

    def y_send(b):
        return remote(Qb.at[b, theirs], Yb.at[b], s_y.at[b], r_y.at[b], inner)

    def y_recv(b):
        return remote(Qb.at[b, mine], Yb.at[b], s_y.at[b], r_y.at[b], inner)

    def f_edge(b):
        return remote(Qb.at[b, mine], region(b, core, mine), s_fe.at[mine, b], r_f.at[mine, b], outer)

    def f_inner(b):
        return remote(Qb.at[b, mine], region(b, core, mine), s_fm.at[b], r_f.at[mine, b], inner)

    def f_on(b):
        return remote(region(b, core, theirs), region(b, core, theirs), s_fe.at[theirs, b], r_f.at[theirs, b], outer)

    def f_recv(b, h):
        return remote(region(b, core, h), region(b, core, h), s_fe.at[h, b], r_f.at[h, b], outer)

    def p_own(b):
        return remote(Qb.at[b, mine], region(b, core, mine), s_p.at[mine, b], r_p.at[mine, b], peer)

    def p_on(b, h):
        return remote(region(b, core, h), region(b, core, h), s_p.at[h, b], r_p.at[h, b], peer)

    def p_recv(b, h):
        return remote(region(b, 1 - core, h), region(b, 1 - core, h), s_p.at[h, b], r_p.at[h, b], peer)

    def local(b):
        return copy(Qb.at[b, mine], region(b, core, mine), s_l.at[b])

    def rows(body):
        def go(i, _):
            body(ds(i * 64, 64))
            return 0
        lax.fori_loop(0, H // 64, go, 0)

    def tick(k):
        q = k % 6
        made = (k < NP1) & (q >= 2)
        before = jnp.where(k >= 1, k - 1, 0)
        had = (k >= 1) & (k <= NP1) & (before % 6 >= 2)
        blk = (before // 6) * 4 + before % 6 - 2

        @pl.when(had)
        def _():
            b = blk
            pair_send(b).wait_recv()

            @pl.when(edge)
            def _():
                def add(rs):
                    for h in range(2):
                        Qb[b, h, rs, :] = (Pb[b, h, rs, :] + Ib[b % 2, h, rs, :].astype(f32)).astype(bf)
                rows(add)
                x_send(b, theirs).start()
                x_send(b, mine).start()

            @pl.when(jnp.logical_not(edge))
            def _():
                def add(rs):
                    for h in range(2):
                        Pb[b, h, rs, :] = Pb[b, h, rs, :] + Ib[b % 2, h, rs, :].astype(f32)
                rows(add)

        @pl.when(made)
        def _():
            pair_send((k // 6) * 4 + q - 2).start()

        v = jnp.where(k >= K0, (k - K0) * 4, 0)
        due = (k >= K0) & (v % 9 < 4) & (k < LAST)
        m_main = v // 9
        steady = due
        m = jnp.where(steady, m_main, k - LAST + 16)
        go = steady | (k >= LAST)

        @pl.when(go & jnp.logical_not(edge))
        def _():
            @pl.when(m < NB)
            def _():
                b = m
                x_send(b, theirs).wait_recv()

                def add(rs):
                    Qb[b, theirs, rs, :] = (Pb[b, theirs, rs, :] + Qb[b, theirs, rs, :].astype(f32)).astype(bf)
                rows(add)
                y_send(b).start()

            @pl.when((m >= 1) & (m <= NB))
            def _():
                b = m - 1
                x_send(b, mine).wait_recv()
                y_recv(b).wait_recv()

                def add(rs):
                    Qb[b, mine, rs, :] = (Pb[b, mine, rs, :] + Qb[b, mine, rs, :].astype(f32)
                                          + Yb[b, rs, :].astype(f32)).astype(bf)
                rows(add)
                f_inner(b).start()
                f_edge(b).start()
                p_own(b).start()
                local(b).start()

            @pl.when((m >= 2) & (m <= NB + 1))
            def _():
                b = m - 2
                f_recv(b, theirs).wait_recv()
                f_on(b).start()
                p_on(b, theirs).start()

        @pl.when(go & edge & (m >= 3) & (m <= NB + 2))
        def _():
            b = m - 3
            for h in range(2):
                f_recv(b, h).wait_recv()
                p_on(b, h).start()

    def trip(k, _):
        slot = k % 2
        is_a, is_b, is_w = kind(k)
        next_a, next_b, next_w = kind(k + 1)
        r = k // 6

        @pl.when(is_a)
        def _():
            @pl.when(k % 6 == 0)
            def _():
                wait(in_loads(r))

                @pl.when(r > 0)
                def _():
                    outs_g(r - 1)[0].wait()
            wait(loads_a(k, slot))

        @pl.when(is_b)
        def _():
            wait(loads_b(k, slot))

            @pl.when(k % 6 == 3)
            def _():
                outs_g(r)[1].wait()

                @pl.when(r < 3)
                def _():
                    start(in_loads(r + 1)[1:])

        @pl.when(is_w)
        def _():
            wait(loads_w(k, slot))

        @pl.when(next_a)
        def _():
            start(loads_a(k + 1, 1 - slot))

        @pl.when(next_b)
        def _():
            start(loads_b(k + 1, 1 - slot))

        @pl.when(k == NP1 - 1)
        def _():
            outs_g(3)[0].wait()

        @pl.when(next_w)
        def _():
            start(loads_w(k + 1, 1 - slot))

        @pl.when(is_a)
        def _():
            i = k % 6
            sub = 512
            for n in range(N // sub):
                h = lax.dot_general(dyb[...], W[slot, pl.ds(n * sub, sub), :], NT, preferred_element_type=f32)
                cs, cs2 = ds(i * N + n * sub, sub), ds(F + i * N + n * sub, sub)
                g, u = gub[0, :, cs].astype(f32), gub[1, :, cs].astype(f32)
                sg = jax.nn.sigmoid(g)
                sl = g * sg
                gub[0, :, cs] = (sl * u).astype(bf)
                dgb[:, cs2] = (h * sl).astype(bf)
                dgb[:, cs] = ((h * u) * (sg + sl * (1.0 - sg))).astype(bf)

            @pl.when(i == 1)
            def _():
                start(outs_g(r))

                @pl.when(r < 3)
                def _():
                    in_loads(r + 1)[0].start()

        @pl.when(is_b)
        def _():
            b = r * 4 + k % 6 - 2
            s = b % 2

            @pl.when(b >= 2)
            def _():
                pair_send(b).wait_send()
            d = lax.dot_general(dgb[...], W[slot], NT, preferred_element_type=f32)
            for h in range(2):
                lo, hi = d[:H, h * R:(h + 1) * R], d[H:, h * R:(h + 1) * R]
                Pb[b, h] = jnp.where(core == 0, lo, hi)
                Sb[s, h] = jnp.where(core == 0, hi, lo).astype(bf)

        @pl.when(is_w)
        def _():
            @pl.when(k >= NP1 + 2)
            def _():
                wait(outs_w(k - 2, dwg))
            sub = 512
            for n in range(N // sub):
                s1 = lax.dot_general(W[slot, :, 0:N], W[slot, :, pl.ds(2 * N + n * sub, sub)], TN, preferred_element_type=f32)
                s2 = lax.dot_general(W[slot, :, N:2 * N], W[slot, :, pl.ds(3 * N + n * sub, sub)], TN, preferred_element_type=f32)
                s = (s1 + s2).astype(bf)
                for h in range(2):
                    dyb[:, ds(slot * 2 * N + h * N + n * sub, sub)] = s[h * R:(h + 1) * R]
            j = (k - NP1) % 4

            @pl.when(j < 2)
            def _():
                start(outs_w(k, dwg))

            @pl.when(j >= 2)
            def _():
                start(outs_w(k, dwu))

        tick(k)
        return 0

    lax.fori_loop(0, END, trip, 0)

    for k in (LAST - 2, LAST - 1):
        wait(outs_w(k, dwu))
    for s in range(2):
        pair_send(s).wait_send()

    def finish(b, _):
        for h in range(2):
            p_recv(b, h).wait_recv()
            p_on(b, h).wait_send()

        @pl.when(edge)
        def _():
            for h in range(2):
                x_send(b, h).wait_send()

        @pl.when(jnp.logical_not(edge))
        def _():
            y_send(b).wait_send()
            f_edge(b).wait_send()
            f_inner(b).wait_send()
            f_on(b).wait_send()
            local(b).wait()
        return 0

    lax.fori_loop(0, NB, finish, 0)


def run_a(x, dy, gate, up, wg, wu, wd):
    S = jax.ShapeDtypeStruct
    dma = pltpu.SemaphoreType.DMA
    return pl.pallas_call(
        kernel_a,
        in_specs=[ANY] * 7,
        out_specs=[ANY] * 5,
        out_shape=[S((T, 2 * F), bf), S((T, F), bf), S((D, F), bf), S((D, F), bf), S((T, D), bf)],
        scratch_shapes=[
            pltpu.VMEM((2, N, D), bf), pltpu.VMEM((R, D), bf), pltpu.VMEM((2, R, F), bf),
            pltpu.VMEM((R, 2 * F), bf),
            pltpu.VMEM((NB, 2, H, R), f32), pltpu.VMEM((NB, 2, H, R), bf), pltpu.VMEM((NB, H, R), bf),
            pltpu.VMEM((2, 2, H, R), bf), pltpu.VMEM((2, 2, H, R), bf),
            dma((2, 4)), dma((3,)), dma((2,)), dma((2, 2)),
            dma((2,)), dma((2,)), dma((2, NB)), dma((2, NB)), dma((NB,)), dma((NB,)),
            dma((2, NB)), dma((2, NB)), dma((NB,)), dma((2, NB)), dma((2, NB)), dma((NB,)),
        ],
        compiler_params=pltpu.CompilerParams(vmem_limit_bytes=67043328, collective_id=0, has_side_effects=True),
    )(x, dy, gate, up, wg, wu, wd)


def kernel_c(hid, dy, dxa, dga, dua, out, dx, dg, du, bx, bg, bu, semi, semo):
    s = pl.program_id(0)
    n = pl.num_programs(0)

    def ins(i):
        m = i % 3
        return [copy(dxa.at[ds(i * 256, 256), :], bx.at[m], semi.at[m, 0]),
                copy(dga.at[ds(i * 512, 512), :], bg.at[m], semi.at[m, 1]),
                copy(dua.at[ds(i * 512, 512), :], bu.at[m], semi.at[m, 2])]

    def outs(i):
        m = i % 3
        return [copy(bx.at[m], dx.at[ds(i * 256, 256), :], semo.at[m, 0]),
                copy(bg.at[m], dg.at[ds(i * 512, 512), :], semo.at[m, 1]),
                copy(bu.at[m], du.at[ds(i * 512, 512), :], semo.at[m, 2])]

    @pl.when(s == 0)
    def _():
        start(ins(0))

    @pl.when(s >= 2)
    def _():
        wait(outs(s - 2))

    @pl.when(s + 1 < n)
    def _():
        start(ins(s + 1))
    wait(ins(s))
    start(outs(s))
    out[...] = lax.dot_general(hid[...], dy[...], TN, preferred_element_type=f32).astype(bf)

    @pl.when(s == n - 1)
    def _():
        wait(outs(s - 1))
        wait(outs(s))


def run_c(hid, dy, dxa, dga, dua):
    S = jax.ShapeDtypeStruct
    return pl.pallas_call(
        kernel_c,
        grid=(8,),
        in_specs=[pl.BlockSpec((T, N), lambda s: (0, s // 4)), pl.BlockSpec((T, N), lambda s: (0, s % 4)), ANY, ANY, ANY],
        out_specs=[pl.BlockSpec((N, N), lambda s: (s // 4, s % 4)), ANY, ANY, ANY],
        out_shape=[S((F, D), bf), S((T, D), bf), S((D, F), bf), S((D, F), bf)],
        scratch_shapes=[pltpu.VMEM((3, 256, D), bf), pltpu.VMEM((3, 512, F), bf), pltpu.VMEM((3, 512, F), bf),
                        pltpu.SemaphoreType.DMA((3, 3)), pltpu.SemaphoreType.DMA((3, 3))],
        compiler_params=pltpu.CompilerParams(vmem_limit_bytes=60 * 2**20),
    )(hid, dy, dxa, dga, dua)


def solution(mesh):
    def step(x, dy, gate, up, wg, wu, wd):
        _, hid, dga, dua, dxa = run_a(x, dy, gate, up, wg, wu, wd)
        dwd, dx, dwg, dwu = run_c(hid, dy, dxa, dga, dua)
        return dx, dwg, dwu, dwd

    tokens, columns, rows = P("dp", None), P(None, "tp"), P("tp", None)
    return jax.shard_map(
        step,
        mesh=mesh,
        in_specs=(tokens, tokens, P("dp", "tp"), P("dp", "tp"), columns, columns, rows),
        out_specs=(tokens, P("dp", "tp"), P("dp", "tp"), P(("dp", "tp"), None)),
        check_vma=False,
    )
```

time: 528 us -> 322 us (0.61); the launches traced: 519 us -> 322 us
  Pallas kernels: 0 us -> 321 us
  matrix products: 292 us -> 0 us
  waiting for transfers between devices: 154 us -> 0 us
  local copies, waits for them, and re-layouts: 58.9 us -> 0 us
  between operations: 14.5 us -> 0.8 us
    pallas_call x0 -> x2, Pallas kernels: none -> 321 us  [the longest x1 259 us: run_a(): pl.pallas_call(kernel_a, in_specs=[ANY] * 7, out_specs=[ANY] * 5, out_sha...]
    dot_general x6 -> x0, matrix products: 292 us -> none  [the longest x1 58.1 us: step(): jnp.dot(d_up, w_up.T, preferred_element_type=jnp.float32)]
    psum x1 -> x0, waiting for transfers between devices: 154 us -> none  [step(): dx = lax.psum(term.astype(jnp.bfloat16), 'tp')]
    unnamed x3 -> x0, local copies, waits for them, and re-layouts: 58.9 us -> none
  transfers between devices with their start and end apart: 1 -> 0, of which waited for: 1 -> 0; matrix products, arithmetic and copies ran while one was open for 35% -> 0% of each run, Pallas kernels for 0% -> 0%
where the time goes in v1:
time: 322 us
  Pallas kernels  321 us (100%)
    pallas_call x1, Pallas kernels, run_a(): pl.pallas_call(kernel_a, in_specs=[ANY] * 7, out_specs=[ANY] * 5, out_sha...  259 us
    pallas_call x1, Pallas kernels, run_c(): pl.pallas_call(kernel_c, grid=(8,), in_specs=[pl.BlockSpec((T, N), lambda...  62.5 us

profile of v1, /device:TPU:0, one launch (start us, length us, event | category | flops | bytes accessed | tf_op | source)
XLA Modules:
  0.0 322.3 jit_solution(9615935347360443807)
XLA Ops:
  0.6 258.9 %shard_map.102 = (bf16[2048,4096]{1,0:T(8,128)(2,1)}, bf16[2048,2048]{1,0:T(8,128)(2,1)}, bf16[4096,2048]{1,0:T(8,128)(2,1)}, bf16[4096,2048]{1,0:T(8,128)(2,1)}, bf16[2048,4096]{1,0:T(8,128)(2,1)}) custom-call(bf16[2048,4096]{1,0:T(8,128)(2,1)} %x.1, bf16[2048,4096]{1,0:T(8,128)(2,1)} %dy.3, bf16[2048,2048]{1,0:T(8,128)(2,1)} %gate.1, ...), custom_call_target="tpu_custom_call" | custom-call | tf_op jit(solution)/shard_map/pallas_call | solution.py:377
  259.6 62.5 %shard_map.103 = (bf16[2048,4096]{1,0:T(8,128)(2,1)}, bf16[2048,4096]{1,0:T(8,128)(2,1)}, bf16[4096,2048]{1,0:T(8,128)(2,1)}, bf16[4096,2048]{1,0:T(8,128)(2,1)}) custom-call(bf16[2048,2048]{1,0:T(8,128)(2,1)} %get-tuple-element.12.hid, bf16[2048,4096]{1,0:T(8,128)(2,1)} %dy.3, bf16[2048,4096]{1,0:T(8,128)(2,1)} %get-tuple-element.13.dxa, ...), custom_call_target="tpu_custom_call" | custom-call | tf_op jit(solution)/shard_map/pallas_call | solution.py:434

commit v2 on v0

v2 whole, which is shorter than its diff:
```python
import jax
import jax.numpy as jnp
from jax import lax
from jax.experimental import pallas as pl
from jax.experimental.pallas import tpu as pltpu
from jax.sharding import PartitionSpec as P

f32, bf = jnp.float32, jnp.bfloat16
NT = (((1,), (1,)), ((), ()))
TN = (((0,), (0,)), ((), ()))
MESH = pl.DeviceIdType.MESH
ANY = pl.BlockSpec(memory_space=pl.ANY)

T, D, F = 2048, 4096, 2048
R = 512
N = 1024
H = R // 2
NP1 = 24
NW = 16
NB = 16
K0 = 4
LAST = NP1 + NW
NUM, DEN = 25, 23
LAG = 4
ELAG = 7
FL = 2
Q = H // 2
NP = 2 * NB
TAIL = 2
KEEP = NP - 2 * TAIL


def ds(start, size):
    return pl.ds(start if isinstance(start, int) else pl.multiple_of(start, size), size)


def copy(a, b, s):
    return pltpu.make_async_copy(a, b, s)


def start(copies):
    for c in copies:
        c.start()


def wait(copies):
    for c in copies:
        c.wait()


def kernel_a(x, dy, gate, up, wg, wu, wd, dgu, hid, dwg, dwu, dx, fin,
             W, dyb, gub, dgb, Pb, Qb, Yb, Ib, Sb,
             semw, semi, semo, semd, r_i, s_i, r_x, s_x, r_y, s_y, r_f, s_fe, s_fm, r_p, s_p, s_l, r_pf, s_pf):
    t = lax.axis_index("tp")
    z, core = t // 2, t % 2
    peer = z * 2 + 1 - core
    edge = (z == 0) | (z == 3)
    outer = jnp.where(z < 2, core, 6 + core)
    inner = jnp.where(z < 2, 4 + core, 2 + core)
    mine = jnp.where(z < 2, 0, 1)
    theirs = 1 - mine
    middle = jnp.where(z < 2, 2 + core, 4 + core)

    def remote(a, b, s, r, to):
        return pltpu.make_async_remote_copy(a, b, s, r, device_id={"tp": to}, device_id_type=MESH)

    def loads_a(k, slot):
        i = k % 6
        return [copy(wd.at[ds(i * N, N), :], W.at[slot], semw.at[slot, 0])]

    def loads_b(k, slot):
        j = k % 6 - 2
        return [copy(wg.at[ds(j * N, N), :], W.at[slot, :, pl.ds(0, F)], semw.at[slot, 0]),
                copy(wu.at[ds(j * N, N), :], W.at[slot, :, pl.ds(F, F)], semw.at[slot, 1])]

    def loads_w(k, slot):
        i, j = (k - NP1) // 4, (k - NP1) % 4
        return [copy(x.at[pl.ds(0, N), ds(i * N, N)], W.at[slot, :, pl.ds(0, N)], semw.at[slot, 0]),
                copy(x.at[pl.ds(N, N), ds(i * N, N)], W.at[slot, :, pl.ds(N, N)], semw.at[slot, 1]),
                copy(dgu.at[pl.ds(0, N), ds(j * N, N)], W.at[slot, :, pl.ds(2 * N, N)], semw.at[slot, 2]),
                copy(dgu.at[pl.ds(N, N), ds(j * N, N)], W.at[slot, :, pl.ds(3 * N, N)], semw.at[slot, 3])]

    def part(q, n):
        return pl.ds(q * n, n)

    def loads_dy(r, q, n):
        return [copy(dy.at[ds(r * R + q * n, n), :], dyb.at[part(q, n)], semi.at[0, q])]

    def loads_gate(r, q, n):
        return [copy(gate.at[ds(r * R + q * n, n), :], gub.at[0, part(q, n)], semi.at[1, q])]

    def loads_up(r, q, n):
        return [copy(up.at[ds(r * R + q * n, n), :], gub.at[1, part(q, n)], semi.at[2, q])]

    def loads_gu(r, q, n):
        return loads_gate(r, q, n) + loads_up(r, q, n)

    def outs_g(r, q, n):
        return [copy(dgb.at[part(q, n)], dgu.at[ds(r * R + q * n, n), :], semo.at[0, q])]

    def outs_h(r, q, n):
        return [copy(gub.at[0, part(q, n)], hid.at[ds(r * R + q * n, n), :], semo.at[1, q])]

    def outs_w(k, dst):
        slot, i, j = k % 2, (k - NP1) // 4, (k - NP1) % 2
        return [copy(dyb.at[:, ds(slot * 2 * N + h * N, N)],
                     dst.at[ds(i * N + h * R, R), ds(j * N, N)], semd.at[slot, h]) for h in range(2)]

    start(loads_a(0, 0))
    start(loads_dy(0, 0, R) + loads_gu(0, 0, R))
    barrier = pltpu.get_barrier_semaphore()
    pl.semaphore_signal(barrier, inc=1, device_id={"tp": peer}, device_id_type=MESH)

    @pl.when(edge)
    def _():
        pl.semaphore_signal(barrier, inc=1, device_id={"tp": middle}, device_id_type=MESH)

    @pl.when(jnp.logical_not(edge))
    def _():
        pl.semaphore_signal(barrier, inc=1, device_id={"tp": outer}, device_id_type=MESH)
        pl.semaphore_signal(barrier, inc=1, device_id={"tp": inner}, device_id_type=MESH)
    pl.semaphore_wait(barrier, jnp.where(edge, 2, 3))

    def piece(ref, u, h=None):
        ref = ref.at[u // 2] if h is None else ref.at[u // 2, h]
        return ref.at[ds(u % 2 * Q, Q), :]

    def region(u, c, h):
        b = u // 2
        return dx.at[ds((b // 4) * R + c * H + u % 2 * Q, Q), ds((b % 4) * N + h * R, R)]

    def pair_send(b):
        s = b % 2
        return remote(Sb.at[s], Ib.at[s], s_i.at[s], r_i.at[s], peer)

    def x_send(u, h):
        return remote(piece(Qb, u, h), piece(Qb, u, h), s_x, r_x.at[h, u], middle)

    def y_send(u):
        return remote(piece(Qb, u, theirs), piece(Yb, u), s_y, r_y.at[u], inner)

    def f_edge(u):
        return remote(piece(Qb, u, mine), region(u, core, mine), s_fe, r_f.at[mine, u], outer)

    def f_inner(u):
        return remote(piece(Qb, u, mine), region(u, core, mine), s_fm, r_f.at[mine, u], inner)

    def f_on(u, h):
        a = region(u, core, h)
        return remote(a, a, s_fe, r_f.at[h, u], outer)

    def p_own(u):
        return remote(piece(Qb, u, mine), region(u, core, mine), s_p, r_p, peer)

    def p_on(u, h):
        a = region(u, core, h)
        return remote(a, a, s_p, r_p, peer)

    def fin_at(u, c):
        v = u - KEEP
        return fin.at[v // 2, ds(c * H + v % 2 * Q, Q), :]

    def p_fin(u):
        return remote(piece(Qb, u, mine), fin_at(u, core), s_pf, r_pf, peer)

    def local_fin(u):
        return copy(piece(Qb, u, mine), fin_at(u, core), s_l)

    def local(u):
        return copy(piece(Qb, u, mine), region(u, core, mine), s_l)

    def pair(b):
        pair_send(b).wait_recv()

        @pl.when(edge)
        def _():
            for g in range(2):
                rs = pl.ds(g * Q, Q)
                for h in range(2):
                    Qb[b, h, rs, :] = (Pb[b, h, rs, :] + Ib[b % 2, h, rs, :].astype(f32)).astype(bf)
            for g in range(2):
                x_send(2 * b + g, theirs).start()
                x_send(2 * b + g, mine).start()

        @pl.when(jnp.logical_not(edge))
        def _():
            for g in range(2):
                rs = pl.ds(g * Q, Q)
                for h in range(2):
                    Pb[b, h, rs, :] = Pb[b, h, rs, :] + Ib[b % 2, h, rs, :].astype(f32)

    def pass_on(u):
        b, rs = u // 2, ds(u % 2 * Q, Q)
        x_send(u, theirs).wait_recv()
        Qb[b, theirs, rs, :] = (Pb[b, theirs, rs, :] + Qb[b, theirs, rs, :].astype(f32)).astype(bf)
        y_send(u).start()

    def finish(u):
        b, rs = u // 2, ds(u % 2 * Q, Q)
        x_send(u, mine).wait_recv()
        y_send(u).wait_recv()
        Qb[b, mine, rs, :] = (Pb[b, mine, rs, :] + Qb[b, mine, rs, :].astype(f32) + Yb[b, rs, :].astype(f32)).astype(bf)

        @pl.when(u < KEEP)
        def _():
            f_inner(u).start()
            f_edge(u).start()
            p_own(u).start()
            local(u).start()

        @pl.when(u >= KEEP)
        def _():
            p_fin(u).start()
            local_fin(u).start()

    def hand_on(u):
        f_on(u, theirs).wait_recv()
        f_on(u, theirs).start()
        p_on(u, theirs).start()

    def arrive(u):
        for h in range(2):
            f_on(u, h).wait_recv()
            p_on(u, h).start()

    def tick(k):
        v = jnp.where(k >= K0, (k - K0) * DEN, 0)
        u = v // NUM
        due = (k >= K0) & (v - u * NUM < DEN)

        @pl.when(due & jnp.logical_not(edge))
        def _():
            @pl.when(u < NP)
            def _():
                pass_on(u)

            @pl.when((u >= FL) & (u - FL < NP))
            def _():
                finish(u - FL)

            @pl.when((u >= LAG) & (u - LAG < KEEP))
            def _():
                hand_on(u - LAG)

        @pl.when(due & edge & (u >= ELAG) & (u - ELAG < KEEP))
        def _():
            arrive(u - ELAG)

    def trip_a(r, i):
        slot, k = i, r * 6 + i
        wait(loads_a(k, slot))

        @pl.when(i == 0)
        def _():
            @pl.when(r == 0)
            def _():
                wait(loads_dy(0, 0, R) + loads_gu(0, 0, R))

            @pl.when(r > 0)
            def _():
                for q in range(4):
                    wait(loads_dy(r, q, R // 4) + outs_g(r - 1, q, R // 4))
                for q in range(2):
                    wait(loads_gu(r, q, R // 2))
            start(loads_a(1, 1))

        @pl.when(i == 1)
        def _():
            start(loads_b(2, 0))
        sub = 512
        for n in range(N // sub):
            h = lax.dot_general(dyb[...], W[slot, pl.ds(n * sub, sub), :], NT, preferred_element_type=f32)
            cs, cs2 = ds(i * N + n * sub, sub), ds(F + i * N + n * sub, sub)
            g, u = gub[0, :, cs].astype(f32), gub[1, :, cs].astype(f32)
            sg = jax.nn.sigmoid(g)
            sl = g * sg
            gub[0, :, cs] = (sl * u).astype(bf)
            dgb[:, cs2] = (h * sl).astype(bf)
            dgb[:, cs] = ((h * u) * (sg + sl * (1.0 - sg))).astype(bf)
        @pl.when((i == 0) & (r > 0))
        def _():
            pair(r * 4 - 1)
        tick(k)

    def trip_b(r, j):
        slot, k, b = j % 2, r * 6 + 2 + j, r * 4 + j
        s = b % 2
        wait(loads_b(j + 2, slot))

        @pl.when(j < 3)
        def _():
            start(loads_b(j + 3, 1 - slot))
        for q in range(4):
            @pl.when(j == q)
            def _():
                for o in ((0,), (1,), (2, 3), ())[q]:
                    start(outs_g(r, o, R // 4))
                if q < 2:
                    start(outs_h(r, q, R // 2))

                    @pl.when(r < 3)
                    def _():
                        start(loads_dy(r + 1, q, R // 4) + loads_up(r + 1, q, R // 2))
                else:
                    wait(outs_h(r, q - 2, R // 2))

                    @pl.when(r < 3)
                    def _():
                        start(loads_dy(r + 1, q, R // 4) + loads_gate(r + 1, q - 2, R // 2))
                if q == 3:
                    @pl.when(r < 3)
                    def _():
                        start(loads_a(0, 0))

                    @pl.when(r == 3)
                    def _():
                        for o in range(4):
                            wait(outs_g(3, o, R // 4))
                        start(loads_w(NP1, 0))
        @pl.when(b >= 2)
        def _():
            pair_send(b).wait_send()
        d = lax.dot_general(dgb[...], W[slot], NT, preferred_element_type=f32)
        for h in range(2):
            lo, hi = d[:H, h * R:(h + 1) * R], d[H:, h * R:(h + 1) * R]
            Pb[b, h] = jnp.where(core == 0, lo, hi)
            Sb[s, h] = jnp.where(core == 0, hi, lo).astype(bf)
        @pl.when((j > 0) & (b != 1))
        def _():
            pair(b - 1)
        pair_send(b).start()

        @pl.when(b == 0)
        def _():
            pair(0)
        tick(k)

    def trip_w(t):
        slot, k = t % 2, t + NP1
        wait(loads_w(k, slot))

        @pl.when(t < NW - 1)
        def _():
            start(loads_w(k + 1, 1 - slot))

        @pl.when(t >= 2)
        def _():
            wait(outs_w(k - 2, dwg))
        sub = 512
        for n in range(N // sub):
            s1 = lax.dot_general(W[slot, :, 0:N], W[slot, :, pl.ds(2 * N + n * sub, sub)], TN, preferred_element_type=f32)
            s2 = lax.dot_general(W[slot, :, N:2 * N], W[slot, :, pl.ds(3 * N + n * sub, sub)], TN, preferred_element_type=f32)
            s = (s1 + s2).astype(bf)
            for h in range(2):
                dyb[:, ds(slot * 2 * N + h * N + n * sub, sub)] = s[h * R:(h + 1) * R]
        j = t % 4

        @pl.when(j < 2)
        def _():
            start(outs_w(k, dwg))

        @pl.when(j >= 2)
        def _():
            start(outs_w(k, dwu))
        @pl.when(t == 0)
        def _():
            pair(NB - 1)
        tick(k)

    def each(n, body):
        def go(i, _):
            body(i)
            return 0
        lax.fori_loop(0, n, go, 0)

    def chunk(r):
        each(2, lambda i: trip_a(r, i))
        each(4, lambda j: trip_b(r, j))

    each(4, chunk)
    each(NW, trip_w)

    for k in (LAST - 2, LAST - 1):
        wait(outs_w(k, dwu))

    done = (LAST - 1 - K0) * DEN // NUM

    @pl.when(jnp.logical_not(edge))
    def _():
        for u in range(done + 1, NP + FL):
            if u < NP:
                pass_on(u)
            if u - FL < NP:
                finish(u - FL)
            if u - LAG < KEEP:
                hand_on(u - LAG)

    @pl.when(edge)
    def _():
        for u in range(done - ELAG + 1, KEEP):
            arrive(u)
    for s in range(2):
        pair_send(s).wait_send()

    full, most = pl.ds(0, NB), pl.ds(0, NB - TAIL)

    def all_of(ref, n, s, r):
        return remote(ref.at[n], ref.at[n], s, r, peer)

    both = all_of(Qb, most, s_p, r_p)
    both.wait_recv()
    both.wait_send()

    @pl.when(edge)
    def _():
        all_of(Qb, full, s_x, r_p).wait_send()

    @pl.when(jnp.logical_not(edge))
    def _():
        all_of(Yb, full, s_y, r_p).wait_send()
        all_of(Qb, most, s_fe, r_p).wait_send()
        all_of(Yb, most, s_fm, r_p).wait_send()
        all_of(Yb, pl.ds(0, TAIL), s_pf, r_pf).wait()
        copy(Yb, Yb, s_l).wait()


def run_a(x, dy, gate, up, wg, wu, wd):
    S = jax.ShapeDtypeStruct
    dma = pltpu.SemaphoreType.DMA
    return pl.pallas_call(
        kernel_a,
        in_specs=[ANY] * 7,
        out_specs=[ANY] * 6,
        out_shape=[S((T, 2 * F), bf), S((T, F), bf), S((D, F), bf), S((D, F), bf), S((T, D), bf), S((TAIL, R, R), bf)],
        scratch_shapes=[
            pltpu.VMEM((2, N, D), bf), pltpu.VMEM((R, D), bf), pltpu.VMEM((2, R, F), bf),
            pltpu.VMEM((R, 2 * F), bf),
            pltpu.VMEM((NB, 2, H, R), f32), pltpu.VMEM((NB, 2, H, R), bf), pltpu.VMEM((NB, H, R), bf),
            pltpu.VMEM((2, 2, H, R), bf), pltpu.VMEM((2, 2, H, R), bf),
            dma((2, 4)), dma((3, 4)), dma((2, 4)), dma((2, 2)),
            dma((2,)), dma((2,)), dma((2, NP)), dma(()), dma((NP,)), dma(()),
            dma((2, NP)), dma(()), dma(()), dma(()), dma(()), dma(()), dma(()), dma(()),
        ],
        compiler_params=pltpu.CompilerParams(vmem_limit_bytes=67043328, collective_id=0, has_side_effects=True),
    )(x, dy, gate, up, wg, wu, wd)


SLOTS = 5
STEPS = 8


def kernel_c(hid, dy, dxa, dga, dua, out, dx, dg, du, bx, bg, bu, semi, semo):
    s = pl.program_id(0)
    ahead = 3

    def parts(i, into):
        m = i % SLOTS
        pairs = [(dxa, bx, dx, T // STEPS), (dga, bg, dg, D // STEPS), (dua, bu, du, D // STEPS)]
        if into:
            return [copy(a.at[ds(i * n, n), :], b.at[m], semi.at[m, p]) for p, (a, b, _, n) in enumerate(pairs)]
        return [copy(b.at[m], c.at[ds(i * n, n), :], semo.at[m, p]) for p, (_, b, c, n) in enumerate(pairs)]

    @pl.when(s == 0)
    def _():
        for i in range(ahead):
            start(parts(i, True))

    @pl.when(s >= SLOTS - ahead)
    def _():
        wait(parts(s - SLOTS + ahead, False))

    @pl.when(s + ahead < STEPS)
    def _():
        start(parts(s + ahead, True))
    wait(parts(s, True))
    start(parts(s, False))
    out[...] = lax.dot_general(hid[...], dy[...], TN, preferred_element_type=f32).astype(bf)

    @pl.when(s == STEPS - 1)
    def _():
        for i in range(STEPS - SLOTS + ahead, STEPS):
            wait(parts(i, False))


def run_c(hid, dy, dxa, dga, dua):
    S = jax.ShapeDtypeStruct
    dma = pltpu.SemaphoreType.DMA
    n = D // STEPS
    return pl.pallas_call(
        kernel_c,
        grid=(STEPS,),
        in_specs=[pl.BlockSpec((T, F), lambda s: (0, 0)), pl.BlockSpec((T, n), lambda s: (0, s)), ANY, ANY, ANY],
        out_specs=[pl.BlockSpec((F, n), lambda s: (0, s)), ANY, ANY, ANY],
        out_shape=[S((F, D), bf), S((T, D), bf), S((D, F), bf), S((D, F), bf)],
        scratch_shapes=[pltpu.VMEM((SLOTS, T // STEPS, D), bf), pltpu.VMEM((SLOTS, D // STEPS, F), bf),
                        pltpu.VMEM((SLOTS, D // STEPS, F), bf), dma((SLOTS, 3)), dma((SLOTS, 3))],
        cost_estimate=pl.CostEstimate(flops=2 * T * F * D, bytes_accessed=150 * 2**20, transcendentals=0),
        compiler_params=pltpu.CompilerParams(vmem_limit_bytes=67043328),
    )(hid, dy, dxa, dga, dua)


def kernel_d(dx, fin, near, other, far, out, buf, semi, semo):
    z = lax.axis_index("tp") // 2
    first = D - TAIL * N
    for i in range(4):
        @pl.when(z == i)
        def _():
            for h, a in enumerate(((near, far), (fin, other), (other, fin), (far, near))[i]):
                copy(a, buf.at[h], semi.at[h]).start()
    for h in range(2):
        copy(fin, buf.at[h], semi.at[h]).wait()
        parts = [copy(buf.at[h, b], out.at[pl.ds(T - R, R), pl.ds(first + b * N + h * R, R)], semo.at[h, b]) for b in range(TAIL)]
        start(parts)
    for h in range(2):
        wait([copy(buf.at[h, b], out.at[pl.ds(T - R, R), pl.ds(first + b * N + h * R, R)], semo.at[h, b]) for b in range(TAIL)])


def run_d(dx, *parts):
    dma = pltpu.SemaphoreType.DMA
    return pl.pallas_call(
        kernel_d,
        in_specs=[ANY] * 5,
        out_specs=ANY,
        out_shape=jax.ShapeDtypeStruct((T, D), bf),
        scratch_shapes=[pltpu.VMEM((2, TAIL, R, R), bf), dma((2,)), dma((2, TAIL))],
        input_output_aliases={0: 0},
    )(dx, *parts)


def solution(mesh):
    def step(x, dy, gate, up, wg, wu, wd):
        _, hid, dga, dua, dxa, fin = run_a(x, dy, gate, up, wg, wu, wd)

        def send(to1, to2):
            return lax.ppermute(fin, "tp", [(2 + c, 2 * to1 + c) for c in (0, 1)] + [(4 + c, 2 * to2 + c) for c in (0, 1)])
        near, other, far = send(0, 3), send(2, 1), send(3, 0)
        dwd, dx, dwg, dwu = run_c(hid, dy, dxa, dga, dua)
        dx = run_d(dx, fin, near, other, far)
        return dx, dwg, dwu, dwd

    tokens, columns, rows = P("dp", None), P(None, "tp"), P("tp", None)
    return jax.shard_map(
        step,
        mesh=mesh,
        in_specs=(tokens, tokens, P("dp", "tp"), P("dp", "tp"), columns, columns, rows),
        out_specs=(tokens, P("dp", "tp"), P("dp", "tp"), P(("dp", "tp"), None)),
        check_vma=False,
    )
```

time: 528 us -> 280 us (0.53); the launches traced: 519 us -> 277 us
  matrix products: 292 us -> 0 us
  Pallas kernels: 0 us -> 272 us
  waiting for transfers between devices: 154 us -> 0.01 us
  local copies, waits for them, and re-layouts: 58.9 us -> 0 us
  between operations: 14.5 us -> 0.85 us
    dot_general x6 -> x0, matrix products: 292 us -> none  [the longest x1 58.1 us: step(): jnp.dot(d_up, w_up.T, preferred_element_type=jnp.float32)]
    pallas_call x0 -> x3, Pallas kernels: none -> 272 us  [the longest x1 220 us: run_a(): pl.pallas_call(kernel_a, in_specs=[ANY] * 7, out_specs=[ANY] * 6, out_sha...]
    psum x1 -> x0, waiting for transfers between devices: 154 us -> none  [step(): dx = lax.psum(term.astype(jnp.bfloat16), 'tp')]
    unnamed x3 -> x0, local copies, waits for them, and re-layouts: 58.9 us -> none
  transfers between devices with their start and end apart: 1 -> 3, of which waited for: 1 -> 0; matrix products, arithmetic and copies ran while one was open for 35% -> 0% of each run, Pallas kernels for 0% -> 18%
where the time goes in v2:
time: 280 us; the launch traced here: 277 us
  Pallas kernels  272 us (97%)
  starting transfers between devices  4.26 us (2%)
    pallas_call x1, Pallas kernels, run_a(): pl.pallas_call(kernel_a, in_specs=[ANY] * 7, out_specs=[ANY] * 6, out_sha...  220 us
    pallas_call x1, Pallas kernels, run_c(): pl.pallas_call(kernel_c, grid=(STEPS,), in_specs=[pl.BlockSpec((T, F), la...  49.8 us
  transfers between devices with their start and end apart: 3, of which 0 were waited for; matrix products, arithmetic and copies ran while one was open for 0% of the time, Pallas kernels for 18%

profile of v2, /device:TPU:0, one launch (start us, length us, event | category | flops | bytes accessed | tf_op | source)
XLA Modules:
  0.0 277.1 jit_solution(16587584888466176570)
XLA Ops:
  0.6 219.6 %shard_map.102 = (bf16[2048,4096]{1,0:T(8,128)(2,1)}, bf16[2048,2048]{1,0:T(8,128)(2,1)}, bf16[4096,2048]{1,0:T(8,128)(2,1)}, bf16[4096,2048]{1,0:T(8,128)(2,1)}...) custom-call(bf16[2048,4096]{1,0:T(8,128)(2,1)} %x.1, bf16[2048,4096]{1,0:T(8,128)(2,1)} %dy.3, ...), custom_call_target="tpu_custom_call" | custom-call | tf_op jit(solution)/shard_map/pallas_call | solution.py:430
  220.3 1.3 collective-permute-start
  221.6 1.7 collective-permute-start.1
  223.3 1.3 collective-permute-start.2
  224.6 49.8 %shard_map.103 = (bf16[2048,4096]{1,0:T(8,128)(2,1)}, bf16[2048,4096]{1,0:T(8,128)(2,1)}, bf16[4096,2048]{1,0:T(8,128)(2,1)}, bf16[4096,2048]{1,0:T(8,128)(2,1)}) custom-call(bf16[2048,2048]{1,0:T(8,128)(2,1)} %get-tuple-element.13.hid, bf16[2048,4096]{1,0:T(8,128)(2,1)} %dy.3, bf16[2048,4096]{1,0:T(8,128)(2,1)} %get-tuple-element.14.dxa, ...), custom_call_target="tpu_custom_call" | custom-call | flops 34359738368 | bytes 157286400 | tf_op jit(solution)/shard_map/pallas_call | solution.py:489
  274.4 0.0 collective-permute-done.near
  274.4 0.0 collective-permute-done.1.other
  274.4 0.0 collective-permute-done.2.far
  274.4 2.6 shard_map.104
Async XLA Ops:
  220.3 54.1 %collective-permute-start = (bf16[2,512,512]{2,1,0:T(8,128)(2,1)}, bf16[2,512,512]{2,1,0:T(8,128)(2,1)}, u32[]{:S(2)}, u32[]{:S(2)}) collective-permute-start(bf16[2,512,512]{2,1,0:T(8,128)(2,1)} %get-tuple-element.18.fin), channel_id=1, source_target_pairs={{2,0},{3,1},{4,6},{5,7},{10,8},{11,9},{12,14},{13,15},{18,16},{19,... | collective-permute-start | bytes 3145736 | tf_op jit(solution)/shard_map/ppermute | solution.py:535
  221.6 52.8 %collective-permute-start.1 = (bf16[2,512,512]{2,1,0:T(8,128)(2,1)}, bf16[2,512,512]{2,1,0:T(8,128)(2,1)}, u32[]{:S(2)}, u32[]{:S(2)}) collective-permute-start(bf16[2,512,512]{2,1,0:T(8,128)(2,1)} %get-tuple-element.18.fin), channel_id=1, source_target_pairs={{2,4},{3,5},{4,2},{5,3},{10,12},{11,13},{12,10},{13,11},{18,20},{1... | collective-permute-start | bytes 3145736 | tf_op jit(solution)/shard_map/ppermute | solution.py:535
  223.3 51.1 %collective-permute-start.2 = (bf16[2,512,512]{2,1,0:T(8,128)(2,1)}, bf16[2,512,512]{2,1,0:T(8,128)(2,1)}, u32[]{:S(2)}, u32[]{:S(2)}) collective-permute-start(bf16[2,512,512]{2,1,0:T(8,128)(2,1)} %get-tuple-element.18.fin), channel_id=1, source_target_pairs={{2,6},{3,7},{4,0},{5,1},{10,14},{11,15},{12,8},{13,9},{18,22},{19,... | collective-permute-start | bytes 3145736 | tf_op jit(solution)/shard_map/ppermute | solution.py:535

commit v3 on v2

--- a/solution.py
+++ b/solution.py
@@ -95,6 +95,10 @@
     def loads_gu(r, q, n):
         return loads_gate(r, q, n) + loads_up(r, q, n)
 
+    def first_gu(i):
+        return [copy(a.at[pl.ds(0, R), pl.ds(i * N, N)], gub.at[p, :, pl.ds(i * N, N)], semi.at[1 + p, i])
+                for p, a in enumerate((gate, up))]
+
     def outs_g(r, q, n):
         return [copy(dgb.at[part(q, n)], dgu.at[ds(r * R + q * n, n), :], semo.at[0, q])]
 
@@ -107,7 +111,7 @@
                      dst.at[ds(i * N + h * R, R), ds(j * N, N)], semd.at[slot, h]) for h in range(2)]
 
     start(loads_a(0, 0))
-    start(loads_dy(0, 0, R) + loads_gu(0, 0, R))
+    start(loads_dy(0, 0, R) + first_gu(0) + first_gu(1))
     barrier = pltpu.get_barrier_semaphore()
     pl.semaphore_signal(barrier, inc=1, device_id={"tp": peer}, device_id_type=MESH)
 
@@ -119,7 +123,6 @@
     def _():
         pl.semaphore_signal(barrier, inc=1, device_id={"tp": outer}, device_id_type=MESH)
         pl.semaphore_signal(barrier, inc=1, device_id={"tp": inner}, device_id_type=MESH)
-    pl.semaphore_wait(barrier, jnp.where(edge, 2, 3))
 
     def piece(ref, u, h=None):
         ref = ref.at[u // 2] if h is None else ref.at[u // 2, h]
@@ -254,7 +257,7 @@
         def _():
             @pl.when(r == 0)
             def _():
-                wait(loads_dy(0, 0, R) + loads_gu(0, 0, R))
+                wait(loads_dy(0, 0, R) + first_gu(0))
 
             @pl.when(r > 0)
             def _():
@@ -266,6 +269,9 @@
 
         @pl.when(i == 1)
         def _():
+            @pl.when(r == 0)
+            def _():
+                wait(first_gu(1))
             start(loads_b(2, 0))
         sub = 512
         for n in range(N // sub):
@@ -277,6 +283,10 @@
             gub[0, :, cs] = (sl * u).astype(bf)
             dgb[:, cs2] = (h * sl).astype(bf)
             dgb[:, cs] = ((h * u) * (sg + sl * (1.0 - sg))).astype(bf)
+        @pl.when((i == 1) & (r == 0))
+        def _():
+            pl.semaphore_wait(barrier, jnp.where(edge, 2, 3))
+
         @pl.when((i == 0) & (r > 0))
         def _():
             pair(r * 4 - 1)
@@ -455,31 +465,43 @@
 
     def parts(i, into):
         m = i % SLOTS
-        pairs = [(dxa, bx, dx, T // STEPS), (dga, bg, dg, D // STEPS), (dua, bu, du, D // STEPS)]
+        pairs = [(dga, bg, dg, D // STEPS), (dua, bu, du, D // STEPS)]
+        n, cut = T // STEPS, D - TAIL * N
+        cols = (pl.ds(0, cut), pl.ds(cut, TAIL * N))
         if into:
-            return [copy(a.at[ds(i * n, n), :], b.at[m], semi.at[m, p]) for p, (a, b, _, n) in enumerate(pairs)]
-        return [copy(b.at[m], c.at[ds(i * n, n), :], semo.at[m, p]) for p, (_, b, c, n) in enumerate(pairs)]
+            return ([copy(a.at[ds(i * n, n), :], b.at[m], semi.at[m, p]) for p, (a, b, _, n) in enumerate(pairs)]
+                    + [copy(dxa.at[ds(i * n, n), c], bx.at[m, :, c], semi.at[m, 2 + p]) for p, c in enumerate(cols)])
+        return ([copy(b.at[m], c.at[ds(i * n, n), :], semo.at[m, p]) for p, (_, b, c, n) in enumerate(pairs)]
+                + [copy(bx.at[m, :, c], dx.at[ds(i * n, n), c], semo.at[m, 2 + p]) for p, c in enumerate(cols)])
+
+    def run(op, i, into):
+        copies = parts(i, into)
+        op(copies[:-1])
+
+        @pl.when(i < (T - R) // (T // STEPS))
+        def _():
+            op(copies[-1:])
 
     @pl.when(s == 0)
     def _():
         for i in range(ahead):
-            start(parts(i, True))
+            run(start, i, True)
 
     @pl.when(s >= SLOTS - ahead)
     def _():
-        wait(parts(s - SLOTS + ahead, False))
+        run(wait, s - SLOTS + ahead, False)
 
     @pl.when(s + ahead < STEPS)
     def _():
-        start(parts(s + ahead, True))
-    wait(parts(s, True))
-    start(parts(s, False))
+        run(start, s + ahead, True)
+    run(wait, s, True)
+    run(start, s, False)
     out[...] = lax.dot_general(hid[...], dy[...], TN, preferred_element_type=f32).astype(bf)
 
     @pl.when(s == STEPS - 1)
     def _():
         for i in range(STEPS - SLOTS + ahead, STEPS):
-            wait(parts(i, False))
+            run(wait, i, False)
 
 
 def run_c(hid, dy, dxa, dga, dua):
@@ -493,7 +515,7 @@
         out_specs=[pl.BlockSpec((F, n), lambda s: (0, s)), ANY, ANY, ANY],
         out_shape=[S((F, D), bf), S((T, D), bf), S((D, F), bf), S((D, F), bf)],
         scratch_shapes=[pltpu.VMEM((SLOTS, T // STEPS, D), bf), pltpu.VMEM((SLOTS, D // STEPS, F), bf),
-                        pltpu.VMEM((SLOTS, D // STEPS, F), bf), dma((SLOTS, 3)), dma((SLOTS, 3))],
+                        pltpu.VMEM((SLOTS, D // STEPS, F), bf), dma((SLOTS, 4)), dma((SLOTS, 4))],
         cost_estimate=pl.CostEstimate(flops=2 * T * F * D, bytes_accessed=150 * 2**20, transcendentals=0),
         compiler_params=pltpu.CompilerParams(vmem_limit_bytes=67043328),
     )(hid, dy, dxa, dga, dua)

time: 280 us -> 279 us (level)
  transfers between devices with their start and end apart: 3 -> 3, of which waited for: 0 -> 1; matrix products, arithmetic and copies ran while one was open for 0% -> 0% of each run, Pallas kernels for 18% -> 18%
where the time goes in v3:
time: 279 us; the launch traced here: 277 us
  Pallas kernels  271 us (97%)
  starting transfers between devices  4.26 us (2%)
    pallas_call x1, Pallas kernels, run_a(): pl.pallas_call(kernel_a, in_specs=[ANY] * 7, out_specs=[ANY] * 6, out_sha...  219 us
    pallas_call x1, Pallas kernels, run_c(): pl.pallas_call(kernel_c, grid=(STEPS,), in_specs=[pl.BlockSpec((T, F), la...  49.3 us
  transfers between devices with their start and end apart: 3, of which 1 were waited for; matrix products, arithmetic and copies ran while one was open for 0% of the time, Pallas kernels for 18%

profile of v3, /device:TPU:0, one launch (start us, length us, event | category | flops | bytes accessed | tf_op | source)
XLA Modules:
  0.0 276.8 jit_solution(5651592690636164725)
XLA Ops:
  0.6 219.4 %shard_map.102 = (bf16[2048,4096]{1,0:T(8,128)(2,1)}, bf16[2048,2048]{1,0:T(8,128)(2,1)}, bf16[4096,2048]{1,0:T(8,128)(2,1)}, bf16[4096,2048]{1,0:T(8,128)(2,1)}...) custom-call(bf16[2048,4096]{1,0:T(8,128)(2,1)} %x.1, bf16[2048,4096]{1,0:T(8,128)(2,1)} %dy.3, ...), custom_call_target="tpu_custom_call" | custom-call | tf_op jit(solution)/shard_map/pallas_call | solution.py:440
  220.0 1.3 collective-permute-start
  221.3 1.7 collective-permute-start.1
  223.0 1.3 collective-permute-start.2
  224.3 49.3 %shard_map.103 = (bf16[2048,4096]{1,0:T(8,128)(2,1)}, bf16[2048,4096]{1,0:T(8,128)(2,1)}, bf16[4096,2048]{1,0:T(8,128)(2,1)}, bf16[4096,2048]{1,0:T(8,128)(2,1)}) custom-call(bf16[2048,2048]{1,0:T(8,128)(2,1)} %get-tuple-element.13.hid, bf16[2048,4096]{1,0:T(8,128)(2,1)} %dy.3, bf16[2048,4096]{1,0:T(8,128)(2,1)} %get-tuple-element.14.dxa, ...), custom_call_target="tpu_custom_call" | custom-call | flops 34359738368 | bytes 157286400 | tf_op jit(solution)/shard_map/pallas_call | solution.py:511
  273.6 0.0 collective-permute-done.near
  273.7 0.0 collective-permute-done.1.other
  273.7 0.4 collective-permute-done.2.far
  274.1 2.6 shard_map.104
Async XLA Ops:
  220.0 53.6 %collective-permute-start = (bf16[2,512,512]{2,1,0:T(8,128)(2,1)}, bf16[2,512,512]{2,1,0:T(8,128)(2,1)}, u32[]{:S(2)}, u32[]{:S(2)}) collective-permute-start(bf16[2,512,512]{2,1,0:T(8,128)(2,1)} %get-tuple-element.18.fin), channel_id=1, source_target_pairs={{2,0},{3,1},{4,6},{5,7},{10,8},{11,9},{12,14},{13,15},{18,16},{19,... | collective-permute-start | bytes 3145736 | tf_op jit(solution)/shard_map/ppermute | solution.py:557
  221.3 52.3 %collective-permute-start.1 = (bf16[2,512,512]{2,1,0:T(8,128)(2,1)}, bf16[2,512,512]{2,1,0:T(8,128)(2,1)}, u32[]{:S(2)}, u32[]{:S(2)}) collective-permute-start(bf16[2,512,512]{2,1,0:T(8,128)(2,1)} %get-tuple-element.18.fin), channel_id=1, source_target_pairs={{2,4},{3,5},{4,2},{5,3},{10,12},{11,13},{12,10},{13,11},{18,20},{1... | collective-permute-start | bytes 3145736 | tf_op jit(solution)/shard_map/ppermute | solution.py:557
  223.0 51.0 %collective-permute-start.2 = (bf16[2,512,512]{2,1,0:T(8,128)(2,1)}, bf16[2,512,512]{2,1,0:T(8,128)(2,1)}, u32[]{:S(2)}, u32[]{:S(2)}) collective-permute-start(bf16[2,512,512]{2,1,0:T(8,128)(2,1)} %get-tuple-element.18.fin), channel_id=1, source_target_pairs={{2,6},{3,7},{4,0},{5,1},{10,14},{11,15},{12,8},{13,9},{18,22},{19,... | collective-permute-start | bytes 3145736 | tf_op jit(solution)/shard_map/ppermute | solution.py:557
